TPU v7x, 32 devices: a whole 2x2x4 slice. The times are simulated.
32 devices in a mesh: dp: 4 (over y, x), seq: 4 (over z), grp: 2 (over core).
Axes of the slice: x: 2, y: 2, z: 4, core: 2. Of those that a mesh axis runs over, the one named last changes fastest.
Arguments:
- text_proj: bfloat16 [3, 16, 12, 128, 128], P(None, 'dp', None, ('seq', 'grp')), may hold values from -50 to 50
- image_proj: bfloat16 [3, 16, 12, 160, 128], P(None, ('dp', 'seq'), None, 'grp'), may hold values from -50 to 50
- text_grad: bfloat16 [16, 12, 128, 128], P('dp', None, ('seq', 'grp')), may hold values from -15 to 15
- image_grad: bfloat16 [16, 12, 160, 128], P(('dp', 'seq'), None, 'grp'), may hold values from -15 to 15
- text_lengths: int32 [16], P(('dp', 'seq')), may hold values from 1 to 128
- norm_gains: float32 [2, 2, 128], replicated, may hold values from 0.7 to 5.2
Outputs:
- text_out: bfloat16 [16, 12, 128, 128], P('dp', None, ('seq', 'grp'))
- image_out: bfloat16 [16, 12, 160, 128], P(('dp', 'seq'), None, 'grp')
- text_proj_grad: bfloat16 [3, 16, 12, 128, 128], P(None, 'dp', None, ('seq', 'grp'))
- image_proj_grad: bfloat16 [3, 16, 12, 160, 128], P(None, ('dp', 'seq'), None, 'grp')
- gain_grad: float32 [2, 2, 128], replicated
All inputs are finite; a program needn't handle non-finite values.
Results may differ from a plain program's by a relative error of at most 0.025.
The roundings to bfloat16 on the way count: a program that leaves them out, or rounds other values in their place, can miss the bound.
Values may be sent and summed in bfloat16 or wider, within the bound.
No kernel may reach another device: no remote copies, remote signals or barrier semaphores. Data moves between devices by JAX's collectives and lax.ppermute only.
A program may use at most 64 MiB of HBM per device.

v0:
```python
import jax
import jax.numpy as jnp
from jax import lax
from jax.sharding import PartitionSpec as P

TXT = 128


EPSILON = 1e-06
MASKED = -1e30


def forward(queries, key_rows, value_rows, key_valid):
    factor = queries.shape[-1] ** (-0.5)
    scores = (
        jnp.einsum("nqd,nkd->nqk", queries, key_rows, preferred_element_type=jnp.float32) * factor
    )
    scores = jnp.where(key_valid[:, None, :], scores, MASKED)
    row_max = jnp.max(scores, axis=-1, keepdims=True)
    exponent = jnp.exp(scores - row_max)
    attn_probs = exponent / jnp.sum(exponent, axis=-1, keepdims=True)
    rounded_probs = attn_probs.astype(jnp.bfloat16)
    attn_local = jnp.einsum(
        "nqk,nkd->nqd", rounded_probs, value_rows, preferred_element_type=jnp.float32
    )
    return (attn_probs, rounded_probs, attn_local)


def backward_terms(queries, key_rows, value_rows, attn_probs, rounded_probs, grad_out):
    factor = queries.shape[-1] ** (-0.5)
    grad_value = jnp.einsum(
        "nqk,nqd->nkd", rounded_probs, grad_out, preferred_element_type=jnp.float32
    )
    grad_probs = jnp.einsum(
        "nqd,nkd->nqk", grad_out, value_rows, preferred_element_type=jnp.float32
    )
    row_delta = jnp.sum(attn_probs * grad_probs, axis=-1, keepdims=True)
    grad_scores = (attn_probs * (grad_probs - row_delta) * factor).astype(jnp.bfloat16)
    grad_query = jnp.einsum(
        "nqk,nkd->nqd", grad_scores, key_rows, preferred_element_type=jnp.float32
    ).astype(jnp.bfloat16)
    grad_key = jnp.einsum("nqk,nqd->nkd", grad_scores, queries, preferred_element_type=jnp.float32)
    return (grad_query, grad_key, grad_value)


def sums_item(packed):
    query_one, key_one, value_one, valid_one, grad_one = packed
    attn_probs, rounded_probs, attn_local = forward(
        query_one[None], key_one[None], value_one[None], valid_one[None]
    )
    grad_query, grad_key, grad_value = backward_terms(
        query_one[None], key_one[None], value_one[None], attn_probs, rounded_probs, grad_one[None]
    )
    return (attn_local[0].astype(jnp.bfloat16), grad_query[0], grad_key[0], grad_value[0])


def whole_item(packed):
    attn_local, grad_query, grad_key, grad_value = sums_item(packed)
    return (attn_local, grad_query, grad_key.astype(jnp.bfloat16), grad_value.astype(jnp.bfloat16))


def unit_parts(raw_bf):
    raw_vals = raw_bf.astype(jnp.float32)
    inverse = lax.rsqrt(jnp.mean(raw_vals * raw_vals, axis=-1, keepdims=True) + EPSILON)
    return (raw_vals * inverse, inverse)


def raw_gradient(grad_normed_bf, unit_vec, inverse, gain_rows):
    grad_normed = grad_normed_bf.astype(jnp.float32)
    gain_part = jnp.sum(grad_normed * unit_vec, axis=(1, 2, 3))
    grad_unit = grad_normed * gain_rows
    grad_raw = inverse * (
        grad_unit - unit_vec * jnp.mean(grad_unit * unit_vec, axis=-1, keepdims=True)
    )
    return (grad_raw.astype(jnp.bfloat16), gain_part)


def global_position(local_row, owner_index, text_rows, text_group, image_rows, grp_count):
    text_place = (
        local_row // text_group * grp_count + owner_index
    ) * text_group + local_row % text_group
    image_place = TXT + owner_index * image_rows + (local_row - text_rows)
    return jnp.where(local_row < text_rows, text_place, image_place)


def per_device(text_proj, image_proj, text_grad, image_grad, text_lengths, norm_gains):
    seq_count = lax.axis_size("seq")
    grp_count = lax.axis_size("grp")
    sample_count, head_count, image_rows, head_size = image_grad.shape
    text_group = text_proj.shape[3]
    text_rows = text_group * seq_count
    local_len = text_rows + image_rows
    text_unit, text_inverse = unit_parts(text_proj[:2])
    image_unit, image_inverse = unit_parts(image_proj[:2])
    text_gain = norm_gains[0][:, None, None, None, :]
    image_gain = norm_gains[1][:, None, None, None, :]
    text_stack = jnp.concatenate(
        [(text_unit * text_gain).astype(jnp.bfloat16), text_proj[2:]], axis=0
    )
    image_stack = jnp.concatenate(
        [(image_unit * image_gain).astype(jnp.bfloat16), image_proj[2:]], axis=0
    )
    text_here, text_cot = (
        lax.all_to_all(text_stack, "seq", split_axis=1, concat_axis=3, tiled=True),
        lax.all_to_all(text_grad[None], "seq", split_axis=1, concat_axis=3, tiled=True),
    )
    joint_rows = jnp.concatenate([text_here, image_stack], axis=3)
    cotangent_rows = jnp.concatenate([text_cot[0], image_grad], axis=2)
    key_row = jnp.arange(local_len * grp_count, dtype=jnp.int32)
    key_place = global_position(
        key_row % local_len, key_row // local_len, text_rows, text_group, image_rows, grp_count
    )
    key_valid = (key_place[None, :] >= TXT) | (key_place[None, :] < text_lengths[:, None])
    full_len = local_len * grp_count
    moved_rows, moved_cot = (
        lax.all_to_all(joint_rows, "grp", split_axis=2, concat_axis=3, tiled=True),
        lax.all_to_all(cotangent_rows[None], "grp", split_axis=2, concat_axis=3, tiled=True),
    )
    head_share = moved_rows.shape[2]
    item_count = sample_count * head_share
    flat_rows = moved_rows.reshape(3, item_count, full_len, head_size)
    item_valid = jnp.broadcast_to(
        key_valid[:, None, :], (sample_count, head_share, full_len)
    ).reshape(item_count, full_len)
    attn_local, grad_query, grad_key, grad_value = lax.map(
        whole_item,
        (
            flat_rows[0],
            flat_rows[1],
            flat_rows[2],
            item_valid,
            moved_cot.reshape(item_count, full_len, head_size),
        ),
    )
    results = jnp.stack([attn_local, grad_query, grad_key, grad_value]).reshape(
        4, sample_count, head_share, full_len, head_size
    )
    placed = lax.all_to_all(results, "grp", split_axis=3, concat_axis=2, tiled=True)
    text_back = lax.all_to_all(
        placed[:, :, :, :text_rows], "seq", split_axis=3, concat_axis=1, tiled=True
    )
    image_back = placed[:, :, :, text_rows:]
    text_raw, text_part = raw_gradient(text_back[1:3], text_unit, text_inverse, text_gain)
    image_raw, image_part = raw_gradient(image_back[1:3], image_unit, image_inverse, image_gain)
    partial_value = jnp.stack([text_part, image_part])
    summed_gain = lax.psum(partial_value, ("dp", "seq", "grp"))
    gain_grad = summed_gain / (sample_count * lax.axis_size("dp") * seq_count)
    text_proj_grad = jnp.concatenate([text_raw, text_back[3:]], axis=0)
    image_proj_grad = jnp.concatenate([image_raw, image_back[3:]], axis=0)
    return (text_back[0], image_back[0], text_proj_grad, image_proj_grad, gain_grad)


def solution(mesh):
    placed = (
        P(None, "dp", None, ("seq", "grp"), None),
        P(None, ("dp", "seq"), None, "grp", None),
        P("dp", None, ("seq", "grp"), None),
        P(("dp", "seq"), None, "grp", None),
        P(("dp", "seq")),
        P(),
    )
    return jax.shard_map(
        per_device,
        mesh=mesh,
        in_specs=placed,
        out_specs=(
            P("dp", None, ("seq", "grp"), None),
            P(("dp", "seq"), None, "grp", None),
            P(None, "dp", None, ("seq", "grp"), None),
            P(None, ("dp", "seq"), None, "grp", None),
            P(),
        ),
        check_vma=False,
    )
```

profile of v0, /device:TPU:0, one launch (start us, length us, event | category | flops | bytes accessed | tf_op | source)
XLA Modules:
  0.0 161.2 jit_solution(1333477667918705269)
XLA Ops:
  0.6 6.5 %all-to-all-start.2 = ((bf16[1,4,12,16,128]{4,3,2,0,1:T(8,128)(2,1)}), bf16[1,4,12,16,128]{4,3,2,0,1:T(8,128)(2,1)S(1)}, u32[]{:S(2)}, u32[]{:S(2)}) async-start(bf16[1,4,12,16,128]{4,3,2,0,1:T(8,128)(2,1)} %bitcast.157), calls=%async_computation.2 | async-start | bytes 393216 | tf_op jit(solution)/shard_map/all_to_all | solution.py:105
  7.8 1.3 fusion.56
  9.2 1.3 fusion.54
  12.2 2.4 %all-to-all-done.2 = bf16[1,4,12,16,128]{4,3,2,0,1:T(8,128)(2,1)S(1)} async-done(((bf16[1,4,12,16,128]{4,3,2,0,1:T(8,128)(2,1)}), bf16[1,4,12,16,128]{4,3,2,0,1:T(8,128)(2,1)S(1)}, u32[]{:S(2)}, u32[]{:S(2)}) %all-to-all-start.2) | async-done | bytes 196640 | tf_op jit(solution)/shard_map/all_to_all | solution.py:105
  14.7 4.1 %all_to_all.96 = bf16[1,1,12,144,128]{4,3,1,0,2:T(8,128)(2,1)S(1)} all-to-all(bf16[1,1,12,144,128]{4,3,1,0,2:T(8,128)(2,1)S(1)} %maximum_bitcast_fusion.1), channel_id=1, replica_groups=mesh['dp'=4,'seq'=4,'grp'=2] {'grp'}, dimensions={2} | all-to-all | bytes 884736 | tf_op jit(solution)/shard_map/all_to_all | solution.py:117
  18.8 3.5 %all-to-all-start = ((bf16[3,4,12,16,128]{4,3,2,0,1:T(8,128)(2,1)}), bf16[3,4,12,16,128]{4,3,2,0,1:T(8,128)(2,1)S(1)}, u32[]{:S(2)}, u32[]{:S(2)}) async-start(bf16[3,4,12,16,128]{4,3,2,0,1:T(8,128)(2,1)} %copy.85), calls=%async_computation | async-start | bytes 1179648 | tf_op jit(solution)/shard_map/all_to_all | solution.py:104
  24.0 14.7 %all-to-all-done = bf16[3,4,12,16,128]{4,3,2,0,1:T(8,128)(2,1)S(1)} async-done(((bf16[3,4,12,16,128]{4,3,2,0,1:T(8,128)(2,1)}), bf16[3,4,12,16,128]{4,3,2,0,1:T(8,128)(2,1)S(1)}, u32[]{:S(2)}, u32[]{:S(2)}) %all-to-all-start) | async-done | bytes 589856 | tf_op jit(solution)/shard_map/all_to_all | solution.py:104
  39.0 4.8 %all_to_all.97 = bf16[3,1,12,144,128]{4,3,1,0,2:T(8,128)(2,1)S(1)} all-to-all(bf16[3,1,12,144,128]{4,3,1,0,2:T(8,128)(2,1)S(1)} %maximum_maximum_fusion), channel_id=1, replica_groups=mesh['dp'=4,'seq'=4,'grp'=2] {'grp'}, dimensions={2} | all-to-all | bytes 2654208 | tf_op jit(solution)/shard_map/all_to_all | solution.py:116
  44.9 32.7 %while.16 = (s32[]{:T(128)}, bf16[6,288,128]{2,1,0:T(8,128)(2,1)}, bf16[6,288,128]{2,1,0:T(8,128)(2,1)}, bf16[6,288,128]{2,1,0:T(8,128)(2,1)}, bf16[6,288,128]{2...) while((s32[]{:T(128)}, bf16[6,288,128]{2,1,0:T(8,128)(2,1)}, ...), condition=%wide.region_6.7_spmd, body=%wide.region_2.6_spmd.sunk | while | flops 129290400 | bytes 4506681 | solution.py:125
  45.2 1.1 fusion.116
  56.1 1.1 fusion.116
  61.6 1.1 fusion.116
  63.6 1.1 multiply_reduce_fusion.2
  67.0 1.1 fusion.116
  69.1 1.1 multiply_reduce_fusion.2
  72.5 1.1 fusion.116
  77.5 1.5 maximum_bitcast_fusion
  79.1 1.4 copy.95
  80.4 5.2 %all_to_all.98 = bf16[4,1,6,288,128]{4,0,2,1,3:T(4,128)(2,1)S(1)} all-to-all(bf16[4,1,6,288,128]{4,0,2,1,3:T(4,128)(2,1)S(1)} %copy.95), channel_id=1, replica_groups=mesh['dp'=4,'seq'=4,'grp'=2] {'grp'}, dimensions={3} | all-to-all | bytes 3538944 | tf_op jit(solution)/shard_map/all_to_all | solution.py:138
  86.0 1.6 copy.97
  87.5 4.2 %all-to-all-start.5 = ((bf16[4,1,12,64,128]{4,2,1,0,3:T(8,128)(2,1)}), bf16[4,1,12,64,128]{4,2,1,0,3:T(8,128)(2,1)}, u32[]{:S(2)}, u32[]{:S(2)}) async-start(bf16[4,1,12,64,128]{4,2,1,0,3:T(8,128)(2,1)} %copy.97), calls=%async_computation.5 | async-start | bytes 2097152 | tf_op jit(solution)/shard_map/all_to_all | solution.py:139
  95.1 23.1 %all-to-all-done.5 = bf16[4,1,12,64,128]{4,2,1,0,3:T(8,128)(2,1)} async-done(((bf16[4,1,12,64,128]{4,2,1,0,3:T(8,128)(2,1)}), bf16[4,1,12,64,128]{4,2,1,0,3:T(8,128)(2,1)}, u32[]{:S(2)}, u32[]{:S(2)}) %all-to-all-start.5) | async-done | bytes 786464 | tf_op jit(solution)/shard_map/all_to_all | solution.py:139
  118.2 1.7 %copy.98 = bf16[4,1,12,64,128]{4,3,2,0,1:T(8,128)(2,1)S(1)} copy(bf16[4,1,12,64,128]{4,2,1,0,3:T(8,128)(2,1)} %all-to-all-done.5) | data formatting | bytes 1572864 | tf_op jit(solution)/shard_map/all_to_all | solution.py:139
  120.5 37.9 %psum.7 = f32[2,2,128]{2,1,0:T(2,128)S(1)} all-reduce(f32[2,2,128]{2,1,0:T(2,128)S(1)} %pad_maximum_fusion.3), channel_id=1, replica_groups=mesh['dp'=4,'seq'=4,'grp'=2] {'dp','seq','grp'}, use_global_device_ids=true, to_apply=%region_11.12 | all-reduce | flops 512 | bytes 4096 | tf_op jit(solution)/shard_map/psum | solution.py:146
  (95 shorter events, 36.5 us)
Async XLA Ops:
  0.6 10.5 %copy-start.1 = (bf16[3,4,12,16,128]{4,3,2,1,0:T(8,128)(2,1)S(1)}, bf16[3,4,12,16,128]{4,3,2,1,0:T(8,128)(2,1)}, u32[]{:S(2)}) copy-start(bf16[3,4,12,16,128]{4,3,2,1,0:T(8,128)(2,1)} %param.8) | copy-start | bytes 1769476
  0.6 14.0 %all-to-all-start.2 = ((bf16[1,4,12,16,128]{4,3,2,0,1:T(8,128)(2,1)}), bf16[1,4,12,16,128]{4,3,2,0,1:T(8,128)(2,1)S(1)}, u32[]{:S(2)}, u32[]{:S(2)}) async-start(bf16[1,4,12,16,128]{4,3,2,0,1:T(8,128)(2,1)} %bitcast.157), calls=%async_computation.2 | async-start | bytes 393216 | tf_op jit(solution)/shard_map/all_to_all | solution.py:105
  9.2 5.5 %copy-start.3 = (bf16[1,12,80,128]{3,2,1,0:T(8,128)(2,1)S(1)}, bf16[1,12,80,128]{3,2,1,0:T(8,128)(2,1)}, u32[]{:S(2)}) copy-start(bf16[1,12,80,128]{3,2,1,0:T(8,128)(2,1)} %param.11) | copy-start | bytes 737284
  12.2 10.1 %copy-start = (bf16[3,1,12,80,128]{4,3,2,1,0:T(8,128)(2,1)S(1)}, bf16[3,1,12,80,128]{4,3,2,1,0:T(8,128)(2,1)}, u32[]{:S(2)}) copy-start(bf16[3,1,12,80,128]{4,3,2,1,0:T(8,128)(2,1)} %param.9) | copy-start | bytes 2211844
  18.8 19.9 %all-to-all-start = ((bf16[3,4,12,16,128]{4,3,2,0,1:T(8,128)(2,1)}), bf16[3,4,12,16,128]{4,3,2,0,1:T(8,128)(2,1)S(1)}, u32[]{:S(2)}, u32[]{:S(2)}) async-start(bf16[3,4,12,16,128]{4,3,2,0,1:T(8,128)(2,1)} %copy.85), calls=%async_computation | async-start | bytes 1179648 | tf_op jit(solution)/shard_map/all_to_all | solution.py:104
  43.8 1.0 copy-start.2
  87.5 30.6 %all-to-all-start.5 = ((bf16[4,1,12,64,128]{4,2,1,0,3:T(8,128)(2,1)}), bf16[4,1,12,64,128]{4,2,1,0,3:T(8,128)(2,1)}, u32[]{:S(2)}, u32[]{:S(2)}) async-start(bf16[4,1,12,64,128]{4,2,1,0,3:T(8,128)(2,1)} %copy.97), calls=%async_computation.5 | async-start | bytes 2097152 | tf_op jit(solution)/shard_map/all_to_all | solution.py:139
where the time goes:
time: 163 us; the launch traced here: 161 us
  blocking collectives  51.9 us (32%)
  waiting for transfers between devices  40.2 us (25%)
  matrix products  31 us (19%)
  starting transfers between devices  14.2 us (9%)
  local copies, waits for them, and re-layouts  12.2 us (7%)
  other arithmetic  9.94 us (6%)
    psum x1, blocking collectives, per_device(): summed_gain = lax.psum(partial_value, ('dp', 'seq', 'grp'))  37.9 us
    all_to_all x1, waiting for transfers between devices, per_device(): lax.all_to_all(placed[:, :, :, :text_rows], 'seq', split_axis=3, concat_a...  23.1 us
    all_to_all x1, waiting for transfers between devices, per_device(): lax.all_to_all(text_stack, 'seq', split_axis=1, concat_axis=3, tiled=True)  14.7 us
    dot_general x6, matrix products, backward_terms(): jnp.einsum('nqk,nqd->nkd', rounded_probs, grad_out, preferred_element_typ...  6.74 us
    dot_general x6, matrix products, backward_terms(): jnp.einsum('nqd,nkd->nqk', grad_out, value_rows, preferred_element_type=j...  6.74 us
    all_to_all x1, starting transfers between devices, per_device(): lax.all_to_all(text_grad[None], 'seq', split_axis=1, concat_axis=3, tiled...  6.49 us
    dot_general x6, matrix products, forward(): jnp.einsum('nqk,nkd->nqd', rounded_probs, value_rows, preferred_element_t...  5.55 us
    dot_general x6, matrix products, backward_terms(): jnp.einsum('nqk,nkd->nqd', grad_scores, key_rows, preferred_element_type=...  5.4 us
  transfers between devices with their start and end apart: 3, of which 3 were waited for; matrix products, arithmetic and copies ran while one was open for 6% of the time, Pallas kernels for 0%

commit v1 on v0

--- a/solution.py
+++ b/solution.py
@@ -1,6 +1,10 @@
+import functools
+import math
 import jax
 import jax.numpy as jnp
 from jax import lax
+from jax.experimental import pallas as pl
+from jax.experimental.pallas import tpu as pltpu
 from jax.sharding import PartitionSpec as P
 
 TXT = 128
@@ -83,7 +87,7 @@
     return jnp.where(local_row < text_rows, text_place, image_place)
 
 
-def per_device(text_proj, image_proj, text_grad, image_grad, text_lengths, norm_gains):
+def gathered(text_proj, image_proj, text_grad, image_grad, text_lengths, norm_gains):
     seq_count = lax.axis_size("seq")
     grp_count = lax.axis_size("grp")
     sample_count, head_count, image_rows, head_size = image_grad.shape
@@ -150,6 +154,281 @@
     return (text_back[0], image_back[0], text_proj_grad, image_proj_grad, gain_grad)
 
 
+LOG2E = math.log2(math.e)
+SUBLANES = 16
+
+
+def xor_pairs(count, step):
+    return [(index, index ^ step) for index in range(count)]
+
+
+def peer_list(seq_count, grp_count):
+    half = max(seq_count // 2, 1)
+    steps = [step for step in range(half, seq_count)] + [step for step in range(1, half)]
+    remote = [(step, core) for step in steps for core in range(grp_count)]
+    near = [(0, core) for core in range(1, grp_count)]
+    return [(0, 0)] + remote + near
+
+
+def swap(value, step, core):
+    grp_count = lax.axis_size("grp")
+    if step == 0:
+        return lax.ppermute(value, "grp", xor_pairs(grp_count, core))
+    count = lax.axis_size("seq") * grp_count
+    return lax.ppermute(value, ("seq", "grp"), xor_pairs(count, step * grp_count + core))
+
+
+def pack_body(peers, head_share, chunk_heads, place, text_proj, text_grad, image_proj, image_grad, *rest):
+    chunks = head_share // chunk_heads
+    n_text = len(peers) * chunks
+    text_out, rest = rest[:n_text], rest[n_text:]
+    image_out, sems = rest[:-1], rest[-1]
+    seq_at, grp_at = place[0], place[1]
+    copies = []
+    for chunk in range(chunks):
+        for at, (step, core) in enumerate(peers):
+            sample = seq_at ^ step
+            heads = pl.ds((grp_at ^ core) * head_share + chunk * chunk_heads, chunk_heads)
+            target = text_out[chunk * len(peers) + at]
+            copies.append((text_proj.at[:, sample, heads], target.at[pl.ds(0, 3)]))
+            copies.append((text_grad.at[sample, heads], target.at[3]))
+    for core, target in enumerate(image_out):
+        heads = pl.ds((grp_at ^ core) * head_share, head_share)
+        copies.append((image_proj.at[:, 0, heads], target.at[pl.ds(0, 3)]))
+        copies.append((image_grad.at[0, heads], target.at[3]))
+    started = [
+        pltpu.make_async_copy(source, target, sems.at[at])
+        for at, (source, target) in enumerate(copies)
+    ]
+    for copy in started:
+        copy.start()
+    for copy in started:
+        copy.wait()
+
+
+def unpack_body(peers, head_share, chunk_heads, place, *refs):
+    chunks = head_share // chunk_heads
+    n_text = len(peers) * chunks
+    text_in, refs = refs[:n_text], refs[n_text:]
+    image_in, outs = refs[:-5], refs[-5:]
+    text_out, image_out, text_grad, image_grad, sems = outs
+    seq_at, grp_at = place[0], place[1]
+    copies = []
+    for core, source in enumerate(image_in):
+        heads = pl.ds((grp_at ^ core) * head_share, head_share)
+        copies.append((source.at[0], image_out.at[0, heads]))
+        copies.append((source.at[pl.ds(1, 3)], image_grad.at[:, 0, heads]))
+    for chunk in range(chunks):
+        for at, (step, core) in enumerate(peers):
+            sample = seq_at ^ step
+            heads = pl.ds((grp_at ^ core) * head_share + chunk * chunk_heads, chunk_heads)
+            source = text_in[chunk * len(peers) + at]
+            copies.append((source.at[0], text_out.at[sample, heads]))
+            copies.append((source.at[pl.ds(1, 3)], text_grad.at[:, sample, heads]))
+    started = [
+        pltpu.make_async_copy(source, target, sems.at[at])
+        for at, (source, target) in enumerate(copies)
+    ]
+    for copy in started:
+        copy.start()
+    for copy in started:
+        copy.wait()
+
+
+def matmul(left, right, left_dim, right_dim):
+    return lax.dot_general(
+        left, right, (((left_dim,), (right_dim,)), ((), ())), preferred_element_type=jnp.float32
+    )
+
+
+def attend_body(n_text, head_base, heads, place, gains, *refs):
+    text_in, refs = refs[:n_text], refs[n_text:]
+    image_in, refs = refs[:2], refs[2:]
+    text_out, refs = refs[:n_text], refs[n_text:]
+    image_out, gain_out, gain_sum = refs[:2], refs[2], refs[3]
+    group = text_in[0].shape[2]
+    image_rows = image_in[0].shape[2]
+    text_len = n_text * group
+    size = text_in[0].shape[3]
+    factor = size ** (-0.5)
+    length = place[2]
+    row = lax.broadcasted_iota(jnp.int32, (group, 1), 0)
+    bias = jnp.concatenate(
+        [
+            jnp.where(row + place[3 + at] * group < length, 0.0, -1e30).astype(jnp.float32)
+            for at in range(n_text)
+        ],
+        axis=0,
+    )
+    gain_rows = [[gains[stream, c][None, :] for stream in range(2)] for c in range(2)]
+    gain_sum[...] = jnp.zeros_like(gain_sum)
+
+    def per_stream(values, which):
+        return jnp.concatenate(
+            [values[:text_len] * which[0], values[text_len:] * which[1]], axis=0
+        )
+
+    def head(at, carry):
+        def gather(tensor):
+            return jnp.concatenate(
+                [piece[tensor, at] for piece in text_in]
+                + [piece[tensor, head_base + at] for piece in image_in],
+                axis=0,
+            )
+
+        def norm(c):
+            raw = gather(c).astype(jnp.float32)
+            inverse = lax.rsqrt(jnp.mean(raw * raw, axis=-1, keepdims=True) + EPSILON)
+            unit = raw * inverse
+            return unit, inverse, per_stream(unit, gain_rows[c]).astype(jnp.bfloat16)
+
+        query_unit, query_inverse, query = norm(0)
+        key_unit, key_inverse, key = norm(1)
+        value = gather(2)
+        cotangent = gather(3)
+        scores = matmul(key, query, 1, 1) * (factor * LOG2E)
+        scores = jnp.concatenate([scores[:text_len] + bias, scores[text_len:]], axis=0)
+        exponent = jnp.exp2(scores - jnp.max(scores, axis=0, keepdims=True))
+        probs = exponent * (1.0 / jnp.sum(exponent, axis=0, keepdims=True))
+        rounded = probs.astype(jnp.bfloat16)
+        grad_probs = matmul(value, cotangent, 1, 1)
+        delta = jnp.sum(probs * grad_probs, axis=0, keepdims=True)
+        grad_scores = (probs * (grad_probs - delta) * factor).astype(jnp.bfloat16)
+
+        def scatter(tensor, values):
+            for piece_at, piece in enumerate(text_out):
+                piece[tensor, at] = values[piece_at * group : (piece_at + 1) * group]
+            for piece_at, piece in enumerate(image_out):
+                start = text_len + piece_at * image_rows
+                piece[tensor, head_base + at] = values[start : start + image_rows]
+
+        scatter(0, matmul(rounded, value, 0, 0).astype(jnp.bfloat16))
+        scatter(3, matmul(rounded, cotangent, 1, 0).astype(jnp.bfloat16))
+
+        def raw_gradient(c, grad, unit, inverse):
+            grad = grad.astype(jnp.bfloat16).astype(jnp.float32)
+            product = grad * unit
+            for stream, part in enumerate((product[:text_len], product[text_len:])):
+                gain_sum[stream * 2 + c] += jnp.sum(part.reshape(-1, 8, size), axis=0)
+            mean = jnp.mean(per_stream(product, gain_rows[c]), axis=-1, keepdims=True)
+            result = inverse * (per_stream(grad, gain_rows[c]) - unit * mean)
+            scatter(1 + c, result.astype(jnp.bfloat16))
+
+        raw_gradient(0, matmul(grad_scores, key, 0, 0), query_unit, query_inverse)
+        raw_gradient(1, matmul(grad_scores, query, 1, 0), key_unit, key_inverse)
+        return carry
+
+    lax.fori_loop(0, heads, head, 0)
+    gain_out[...] = jnp.sum(gain_sum[...], axis=1)
+
+
+def in_vmem():
+    return pl.BlockSpec(memory_space=pltpu.VMEM)
+
+
+def in_smem():
+    return pl.BlockSpec(memory_space=pltpu.SMEM)
+
+
+def anywhere():
+    return pl.BlockSpec(memory_space=pl.ANY)
+
+
+def tree_sum(values):
+    while len(values) > 1:
+        values = [values[at] + values[at + 1] for at in range(0, len(values), 2)]
+    return values[0]
+
+
+def total_gain(value):
+    value = value + swap(value, 0, 1)
+    for axis in ("dp", "seq"):
+        count = lax.axis_size(axis)
+        others = [lax.ppermute(value, axis, xor_pairs(count, step)) for step in range(1, count)]
+        value = tree_sum([value] + others)
+    return value
+
+
+def direct(text_proj, image_proj, text_grad, image_grad, text_lengths, norm_gains):
+    seq_count = lax.axis_size("seq")
+    grp_count = lax.axis_size("grp")
+    heads, size = image_grad.shape[1], image_grad.shape[3]
+    group, image_rows = text_proj.shape[3], image_grad.shape[2]
+    head_share = heads // grp_count
+    chunk_heads = head_share
+    peers = peer_list(seq_count, grp_count)
+    n_text = len(peers)
+    seq_at, grp_at = lax.axis_index("seq"), lax.axis_index("grp")
+    sources = [(seq_at ^ step) * grp_count + (grp_at ^ core) for step, core in peers]
+    place = jnp.stack([seq_at, grp_at, text_lengths[0]] + sources).astype(jnp.int32)
+    text_piece = jax.ShapeDtypeStruct((4, chunk_heads, group, size), jnp.bfloat16)
+    image_piece = jax.ShapeDtypeStruct((4, head_share, image_rows, size), jnp.bfloat16)
+    packed = pl.pallas_call(
+        functools.partial(pack_body, peers, head_share, chunk_heads),
+        out_shape=[text_piece] * n_text + [image_piece] * grp_count,
+        in_specs=[in_smem()] + [anywhere()] * 4,
+        out_specs=[in_vmem()] * (n_text + grp_count),
+        scratch_shapes=[pltpu.SemaphoreType.DMA((2 * (n_text + grp_count),))],
+        name="pack",
+    )(place, text_proj, text_grad, image_proj, image_grad)
+    text_sent, image_sent = packed[:n_text], packed[n_text:]
+    text_here = [text_sent[0]] + [
+        swap(value, step, core) for value, (step, core) in zip(text_sent[1:], peers[1:])
+    ]
+    image_here = [image_sent[0], swap(image_sent[1], 0, 1)]
+    attended = pl.pallas_call(
+        functools.partial(attend_body, n_text, 0, chunk_heads),
+        out_shape=[text_piece] * n_text
+        + [image_piece] * grp_count
+        + [jax.ShapeDtypeStruct((4, size), jnp.float32)],
+        in_specs=[in_smem()] + [in_vmem()] * (1 + n_text + grp_count),
+        out_specs=[in_vmem()] * (n_text + grp_count + 1),
+        scratch_shapes=[pltpu.VMEM((4, 8, size), jnp.float32)],
+        name="attend",
+    )(place, norm_gains, *text_here, *image_here)
+    text_done, image_done = attended[:n_text], attended[n_text : n_text + grp_count]
+    text_back = [text_done[0]] + [
+        swap(value, step, core) for value, (step, core) in zip(text_done[1:], peers[1:])
+    ]
+    image_back = [image_done[0], swap(image_done[1], 0, 1)]
+    gain_sum = total_gain(attended[-1])
+    gain_grad = gain_sum.reshape(2, 2, size) / (
+        text_grad.shape[0] * lax.axis_size("dp")
+    )
+    outs = pl.pallas_call(
+        functools.partial(unpack_body, peers, head_share, chunk_heads),
+        out_shape=[
+            jax.ShapeDtypeStruct(value.shape, jnp.bfloat16)
+            for value in (text_grad, image_grad, text_proj, image_proj)
+        ],
+        in_specs=[in_smem()] + [in_vmem()] * (n_text + grp_count),
+        out_specs=[anywhere()] * 4,
+        scratch_shapes=[pltpu.SemaphoreType.DMA((2 * (n_text + grp_count),))],
+        name="unpack",
+    )(place, *text_back, *image_back)
+    return (*outs, gain_grad)
+
+
+def power_of_two(count):
+    return count & (count - 1) == 0
+
+
+def per_device(text_proj, image_proj, text_grad, image_grad, text_lengths, norm_gains):
+    seq_count, grp_count = lax.axis_size("seq"), lax.axis_size("grp")
+    aligned = text_proj.shape[3] % SUBLANES == 0 and image_proj.shape[3] % SUBLANES == 0
+    fits = (
+        aligned
+        and grp_count == 2
+        and seq_count <= 8
+        and power_of_two(seq_count)
+        and power_of_two(lax.axis_size("dp"))
+        and image_grad.shape[0] == 1
+        and image_grad.shape[1] % grp_count == 0
+    )
+    form = direct if fits else gathered
+    return form(text_proj, image_proj, text_grad, image_grad, text_lengths, norm_gains)
+
+
 def solution(mesh):
     placed = (
         P(None, "dp", None, ("seq", "grp"), None),

time: 163 us -> 81 us (0.50)
  blocking collectives: 51.9 us -> 0 us
  matrix products: 31 us -> 0 us
  starting transfers between devices: 14.2 us -> 31.9 us
  Pallas kernels: 0 us -> 15 us
  waiting for transfers between devices: 40.2 us -> 29.2 us
  local copies, waits for them, and re-layouts: 12.2 us -> 2.61 us
  other arithmetic: 9.94 us -> 0.61 us
    all_to_all x3 -> x0, waiting for transfers between devices: 40.2 us -> none  [the longest x1 23.1 us: per_device(): lax.all_to_all(placed[:, :, :, :text_rows], 'seq', split_axis=3, concat_a...]
    psum x1 -> x0, blocking collectives: 37.9 us -> none  [per_device(): summed_gain = lax.psum(partial_value, ('dp', 'seq', 'grp'))]
    ppermute x0 -> x23, starting transfers between devices: none -> 31.9 us  [the longest x12 18.6 us: swap(): lax.ppermute(value, ('seq', 'grp'), xor_pairs(count, step * grp_count + c...]
    dot_general x36 -> x0, matrix products: 31 us -> none  [the longest x6 6.74 us: backward_terms(): jnp.einsum('nqk,nqd->nkd', rounded_probs, grad_out, preferred_element_typ...]
    ppermute x0 -> x23, waiting for transfers between devices: none -> 29.2 us  [the longest x12 18.9 us: swap(): lax.ppermute(value, ('seq', 'grp'), xor_pairs(count, step * grp_count + c...]
    pallas_call x0 -> x3, Pallas kernels: none -> 15 us  [the longest x1 8.5 us: direct(): pl.pallas_call(functools.partial(attend_body, n_text, 0, chunk_heads), ou...]
    all_to_all x3 -> x0, starting transfers between devices: 14.2 us -> none  [the longest x1 6.49 us: per_device(): lax.all_to_all(text_grad[None], 'seq', split_axis=1, concat_axis=3, tiled...]
    all_to_all x3 -> x0, blocking collectives: 14 us -> none  [the longest x1 5.16 us: per_device(): lax.all_to_all(results, 'grp', split_axis=3, concat_axis=2, tiled=True)]
  transfers between devices with their start and end apart: 3 -> 23, of which waited for: 3 -> 12; matrix products, arithmetic and copies ran while one was open for 6% -> 1% of each run, Pallas kernels for 0% -> 0%
where the time goes in v1:
time: 81 us; the launch traced here: 80.8 us
  starting transfers between devices  31.9 us (39%)
  waiting for transfers between devices  29.2 us (36%)
  Pallas kernels  15 us (19%)
  local copies, waits for them, and re-layouts  2.61 us (3%)
  between operations  1.46 us (2%)
    ppermute x12, waiting for transfers between devices, swap(): lax.ppermute(value, ('seq', 'grp'), xor_pairs(count, step * grp_count + c...  18.9 us
    ppermute x12, starting transfers between devices, swap(): lax.ppermute(value, ('seq', 'grp'), xor_pairs(count, step * grp_count + c...  18.6 us
    ppermute x6, starting transfers between devices, total_gain(): lax.ppermute(value, axis, xor_pairs(count, step))  11.6 us
    ppermute x6, waiting for transfers between devices, total_gain(): lax.ppermute(value, axis, xor_pairs(count, step))  9.15 us
    pallas_call x1, Pallas kernels, direct(): pl.pallas_call(functools.partial(attend_body, n_text, 0, chunk_heads), ou...  8.5 us
    pallas_call x1, Pallas kernels, direct(): pl.pallas_call(functools.partial(pack_body, peers, head_share, chunk_head...  3.57 us
    pallas_call x1, Pallas kernels, direct(): pl.pallas_call(functools.partial(unpack_body, peers, head_share, chunk_he...  2.91 us
    unnamed x34, local copies, waits for them, and re-layouts  1.93 us
  transfers between devices with their start and end apart: 23, of which 12 were waited for; matrix products, arithmetic and copies ran while one was open for 1% of the time, Pallas kernels for 0%

profile of v1, /device:TPU:0, one launch (start us, length us, event | category | flops | bytes accessed | tf_op | source)
XLA Modules:
  0.0 80.8 jit_solution(16790555001446929095)
XLA Ops:
  2.0 3.6 %pack.1 = (bf16[4,6,16,128]{3,2,1,0:T(8,128)(2,1)}, bf16[4,6,16,128]{3,2,1,0:T(8,128)(2,1)}, bf16[4,6,16,128]{3,2,1,0:T(8,128)(2,1)}, bf16[4,6,16,128]{3,2,1,0:T...) custom-call(s32[11]{0:T(128)} %stack.43.place, ...), custom_call_target="tpu_custom_call" | custom-call | tf_op jit(solution)/shard_map/pack/pallas_call | solution.py:366
  6.1 3.6 %collective-permute-start = (bf16[4,6,16,128]{3,2,1,0:T(8,128)(2,1)}, bf16[4,6,16,128]{3,2,1,0:T(8,128)(2,1)S(1)}, u32[]{:S(2)}, u32[]{:S(2)}) collective-permute-start(bf16[4,6,16,128]{3,2,1,0:T(8,128)(2,1)} %get-tuple-element.31), channel_id=1, source_target_pairs={{0,4},{1,5},{2,6},{3,7},{4,0},{5,1},{6,2},{7,3},{8,12},{9,13},{10,... | collective-permute-start | bytes 294920 | tf_op jit(solution)/shard_map/ppermute | solution.py:178
  9.8 3.7 %collective-permute-start.2 = (bf16[4,6,16,128]{3,2,1,0:T(8,128)(2,1)}, bf16[4,6,16,128]{3,2,1,0:T(8,128)(2,1)S(1)}, u32[]{:S(2)}, u32[]{:S(2)}) collective-permute-start(bf16[4,6,16,128]{3,2,1,0:T(8,128)(2,1)} %get-tuple-element.33), channel_id=1, source_target_pairs={{0,6},{1,7},{2,4},{3,5},{4,2},{5,3},{6,0},{7,1},{8,14},{9,15},{10,... | collective-permute-start | bytes 294920 | tf_op jit(solution)/shard_map/ppermute | solution.py:178
  13.5 8.6 %collective-permute-done.refs_1_ = bf16[4,6,16,128]{3,2,1,0:T(8,128)(2,1)S(1)} collective-permute-done((bf16[4,6,16,128]{3,2,1,0:T(8,128)(2,1)}, bf16[4,6,16,128]{3,2,1,0:T(8,128)(2,1)S(1)}, u32[]{:S(2)}, u32[]{:S(2)}) %collective-permute-start) | collective-permute-done | bytes 98336 | tf_op jit(solution)/shard_map/ppermute | solution.py:178
  22.7 1.0 %collective-permute-done.1.refs_2_ = bf16[4,6,16,128]{3,2,1,0:T(8,128)(2,1)S(1)} collective-permute-done((bf16[4,6,16,128]{3,2,1,0:T(8,128)(2,1)}, bf16[4,6,16,128]{3,2,1,0:T(8,128)(2,1)S(1)}, u32[]{:S(2)}, u32[]{:S(2)}) %collective-permute-start.1) | collective-permute-done | bytes 98336 | tf_op jit(solution)/shard_map/ppermute | solution.py:178
  23.6 0.8 collective-permute-start.5
  24.9 2.0 %collective-permute-done.4.refs_5_ = bf16[4,6,16,128]{3,2,1,0:T(8,128)(2,1)S(1)} collective-permute-done((bf16[4,6,16,128]{3,2,1,0:T(8,128)(2,1)}, bf16[4,6,16,128]{3,2,1,0:T(8,128)(2,1)S(1)}, u32[]{:S(2)}, u32[]{:S(2)}) %collective-permute-start.4) | collective-permute-done | bytes 98336 | tf_op jit(solution)/shard_map/ppermute | solution.py:178
  26.9 1.6 %collective-permute-done.5.refs_6_ = bf16[4,6,16,128]{3,2,1,0:T(8,128)(2,1)S(1)} collective-permute-done((bf16[4,6,16,128]{3,2,1,0:T(8,128)(2,1)}, bf16[4,6,16,128]{3,2,1,0:T(8,128)(2,1)S(1)}, u32[]{:S(2)}, u32[]{:S(2)}) %collective-permute-start.5) | collective-permute-done | bytes 98336 | tf_op jit(solution)/shard_map/ppermute | solution.py:178
  29.3 8.5 %attend.1 = (bf16[4,6,16,128]{3,2,1,0:T(8,128)(2,1)}, bf16[4,6,16,128]{3,2,1,0:T(8,128)(2,1)}, bf16[4,6,16,128]{3,2,1,0:T(8,128)(2,1)}, bf16[4,6,16,128]{3,2,1,0...) custom-call(s32[11]{0:T(128)} %stack.43.place, ...), custom_call_target="tpu_custom_call" | custom-call | tf_op jit(solution)/shard_map/attend/pallas_call | solution.py:379
  38.8 1.2 %collective-permute-done.16 = f32[4,128]{1,0:T(4,128)S(1)} collective-permute-done((f32[4,128]{1,0:T(4,128)S(1)}, f32[4,128]{1,0:T(4,128)S(1)}, u32[]{:S(2)}, u32[]{:S(2)}) %collective-permute-start.16) | collective-permute-done | bytes 2080 | tf_op jit(solution)/shard_map/ppermute | solution.py:176
  40.0 2.7 %collective-permute-start.19 = (f32[4,128]{1,0:T(4,128)S(1)}, f32[4,128]{1,0:T(4,128)S(1)}, u32[]{:S(2)}, u32[]{:S(2)}) collective-permute-start(f32[4,128]{1,0:T(4,128)S(1)} %add.53), channel_id=1, source_target_pairs={{0,24},{8,16},{16,8},{24,0},{1,25},{9,17},{17,9},{25,1},{2,26},{10... | collective-permute-start | bytes 6152 | tf_op jit(solution)/shard_map/ppermute | solution.py:347
  43.5 2.4 %collective-permute-start.8 = (bf16[4,6,16,128]{3,2,1,0:T(8,128)(2,1)}, bf16[4,6,16,128]{3,2,1,0:T(8,128)(2,1)S(1)}, u32[]{:S(2)}, u32[]{:S(2)}) collective-permute-start(bf16[4,6,16,128]{3,2,1,0:T(8,128)(2,1)} %get-tuple-element.41), channel_id=1, source_target_pairs={{0,4},{1,5},{2,6},{3,7},{4,0},{5,1},{6,2},{7,3},{8,12},{9,13},{10,... | collective-permute-start | bytes 294920 | tf_op jit(solution)/shard_map/ppermute | solution.py:178
  46.3 3.6 %collective-permute-start.10 = (bf16[4,6,16,128]{3,2,1,0:T(8,128)(2,1)}, bf16[4,6,16,128]{3,2,1,0:T(8,128)(2,1)S(1)}, u32[]{:S(2)}, u32[]{:S(2)}) collective-permute-start(bf16[4,6,16,128]{3,2,1,0:T(8,128)(2,1)} %get-tuple-element.43), channel_id=1, source_target_pairs={{0,6},{1,7},{2,4},{3,5},{4,2},{5,3},{6,0},{7,1},{8,14},{9,15},{10,... | collective-permute-start | bytes 294920 | tf_op jit(solution)/shard_map/ppermute | solution.py:178
  50.5 4.9 %collective-permute-done.22 = f32[4,128]{1,0:T(4,128)S(1)} collective-permute-done((f32[4,128]{1,0:T(4,128)S(1)}, f32[4,128]{1,0:T(4,128)S(1)}, u32[]{:S(2)}, u32[]{:S(2)}) %collective-permute-start.22) | collective-permute-done | bytes 2080 | tf_op jit(solution)/shard_map/ppermute | solution.py:347
  55.4 6.3 %collective-permute-start.21 = (f32[4,128]{1,0:T(4,128)S(1)}, f32[4,128]{1,0:T(4,128)S(1)}, u32[]{:S(2)}, u32[]{:S(2)}) collective-permute-start(f32[4,128]{1,0:T(4,128)S(1)} %add_add_fusion), channel_id=1, source_target_pairs={{0,4},{2,6},{4,0},{6,2},{1,5},{3,7},{5,1},{7,3},{8,12},{10,14},{12... | collective-permute-start | bytes 6152 | tf_op jit(solution)/shard_map/ppermute | solution.py:347
  61.7 1.6 %collective-permute-done.21 = f32[4,128]{1,0:T(4,128)S(1)} collective-permute-done((f32[4,128]{1,0:T(4,128)S(1)}, f32[4,128]{1,0:T(4,128)S(1)}, u32[]{:S(2)}, u32[]{:S(2)}) %collective-permute-start.21) | collective-permute-done | bytes 2080 | tf_op jit(solution)/shard_map/ppermute | solution.py:347
  63.2 1.4 %collective-permute-start.20 = (f32[4,128]{1,0:T(4,128)S(1)}, f32[4,128]{1,0:T(4,128)S(1)}, u32[]{:S(2)}, u32[]{:S(2)}) collective-permute-start(f32[4,128]{1,0:T(4,128)S(1)} %add_add_fusion), channel_id=1, source_target_pairs={{0,2},{2,0},{4,6},{6,4},{1,3},{3,1},{5,7},{7,5},{8,10},{10,8},{12,... | collective-permute-start | bytes 6152 | tf_op jit(solution)/shard_map/ppermute | solution.py:347
  64.6 2.2 %collective-permute-done.20 = f32[4,128]{1,0:T(4,128)S(1)} collective-permute-done((f32[4,128]{1,0:T(4,128)S(1)}, f32[4,128]{1,0:T(4,128)S(1)}, u32[]{:S(2)}, u32[]{:S(2)}) %collective-permute-start.20) | collective-permute-done | bytes 2080 | tf_op jit(solution)/shard_map/ppermute | solution.py:347
  66.8 1.4 %collective-permute-start.12 = (bf16[4,6,16,128]{3,2,1,0:T(8,128)(2,1)}, bf16[4,6,16,128]{3,2,1,0:T(8,128)(2,1)S(1)}, u32[]{:S(2)}, u32[]{:S(2)}) collective-permute-start(bf16[4,6,16,128]{3,2,1,0:T(8,128)(2,1)} %get-tuple-element.45), channel_id=1, source_target_pairs={{0,2},{1,3},{2,0},{3,1},{4,6},{5,7},{6,4},{7,5},{8,10},{9,11},{10,... | collective-permute-start | bytes 294920 | tf_op jit(solution)/shard_map/ppermute | solution.py:178
  68.2 2.4 %collective-permute-start.13 = (bf16[4,6,16,128]{3,2,1,0:T(8,128)(2,1)}, bf16[4,6,16,128]{3,2,1,0:T(8,128)(2,1)S(1)}, u32[]{:S(2)}, u32[]{:S(2)}) collective-permute-start(bf16[4,6,16,128]{3,2,1,0:T(8,128)(2,1)} %get-tuple-element.46), channel_id=1, source_target_pairs={{0,3},{1,2},{2,1},{3,0},{4,7},{5,6},{6,5},{7,4},{8,11},{9,10},{10,... | collective-permute-start | bytes 294920 | tf_op jit(solution)/shard_map/ppermute | solution.py:178
  71.3 1.9 %collective-permute-done.11.refs_4_ = bf16[4,6,16,128]{3,2,1,0:T(8,128)(2,1)S(1)} collective-permute-done((bf16[4,6,16,128]{3,2,1,0:T(8,128)(2,1)}, bf16[4,6,16,128]{3,2,1,0:T(8,128)(2,1)S(1)}, u32[]{:S(2)}, u32[]{:S(2)}) %collective-permute-start.11) | collective-permute-done | bytes 98336 | tf_op jit(solution)/shard_map/ppermute | solution.py:178
  73.1 1.4 %collective-permute-done.12.refs_5_ = bf16[4,6,16,128]{3,2,1,0:T(8,128)(2,1)S(1)} collective-permute-done((bf16[4,6,16,128]{3,2,1,0:T(8,128)(2,1)}, bf16[4,6,16,128]{3,2,1,0:T(8,128)(2,1)S(1)}, u32[]{:S(2)}, u32[]{:S(2)}) %collective-permute-start.12) | collective-permute-done | bytes 98336 | tf_op jit(solution)/shard_map/ppermute | solution.py:178
  74.5 2.5 %collective-permute-done.13.refs_6_ = bf16[4,6,16,128]{3,2,1,0:T(8,128)(2,1)S(1)} collective-permute-done((bf16[4,6,16,128]{3,2,1,0:T(8,128)(2,1)}, bf16[4,6,16,128]{3,2,1,0:T(8,128)(2,1)S(1)}, u32[]{:S(2)}, u32[]{:S(2)}) %collective-permute-start.13) | collective-permute-done | bytes 98336 | tf_op jit(solution)/shard_map/ppermute | solution.py:178
  77.9 2.9 %unpack.1 = (bf16[4,12,16,128]{3,2,1,0:T(8,128)(2,1)}, bf16[1,12,80,128]{3,2,1,0:T(8,128)(2,1)}, bf16[3,4,12,16,128]{4,3,2,1,0:T(8,128)(2,1)}, bf16[3,1,12,80,128]{4,3,2,1,0:T(8,128)(2,1)}) custom-call(s32[11]{0:T(128)} %stack.43.place, bf16[4,6,16,128]{3,2,1,0:T(8,128)(2,1)} %get-tuple-element.40.refs_0_, bf16[4,6,16,128]{3,2,1,0:T(8,128)(2,1)} %copy-done.9, ...), custom_call_target="tpu_custom_call" | custom-call | tf_op jit(solution)/shard_map/unpack/pallas_call | solution.py:398
  (63 shorter events, 7.3 us)
Async XLA Ops:
  5.6 23.0 %collective-permute-start.7 = (bf16[4,6,80,128]{3,2,1,0:T(8,128)(2,1)}, bf16[4,6,80,128]{3,2,1,0:T(8,128)(2,1)S(1)}, u32[]{:S(2)}, u32[]{:S(2)}) collective-permute-start(bf16[4,6,80,128]{3,2,1,0:T(8,128)(2,1)} %get-tuple-element.39), channel_id=1, source_target_pairs={{0,1},{1,0},{2,3},{3,2},{4,5},{5,4},{6,7},{7,6},{8,9},{9,8},{10,11... | collective-permute-start | bytes 1474568 | tf_op jit(solution)/shard_map/ppermute | solution.py:176
  6.1 15.9 %collective-permute-start = (bf16[4,6,16,128]{3,2,1,0:T(8,128)(2,1)}, bf16[4,6,16,128]{3,2,1,0:T(8,128)(2,1)S(1)}, u32[]{:S(2)}, u32[]{:S(2)}) collective-permute-start(bf16[4,6,16,128]{3,2,1,0:T(8,128)(2,1)} %get-tuple-element.31), channel_id=1, source_target_pairs={{0,4},{1,5},{2,6},{3,7},{4,0},{5,1},{6,2},{7,3},{8,12},{9,13},{10,... | collective-permute-start | bytes 294920 | tf_op jit(solution)/shard_map/ppermute | solution.py:178
  9.8 13.9 %collective-permute-start.1 = (bf16[4,6,16,128]{3,2,1,0:T(8,128)(2,1)}, bf16[4,6,16,128]{3,2,1,0:T(8,128)(2,1)S(1)}, u32[]{:S(2)}, u32[]{:S(2)}) collective-permute-start(bf16[4,6,16,128]{3,2,1,0:T(8,128)(2,1)} %get-tuple-element.32), channel_id=1, source_target_pairs={{0,5},{1,4},{2,7},{3,6},{4,1},{5,0},{6,3},{7,2},{8,13},{9,12},{10,... | collective-permute-start | bytes 294920 | tf_op jit(solution)/shard_map/ppermute | solution.py:178
  9.8 14.6 %collective-permute-start.2 = (bf16[4,6,16,128]{3,2,1,0:T(8,128)(2,1)}, bf16[4,6,16,128]{3,2,1,0:T(8,128)(2,1)S(1)}, u32[]{:S(2)}, u32[]{:S(2)}) collective-permute-start(bf16[4,6,16,128]{3,2,1,0:T(8,128)(2,1)} %get-tuple-element.33), channel_id=1, source_target_pairs={{0,6},{1,7},{2,4},{3,5},{4,2},{5,3},{6,0},{7,1},{8,14},{9,15},{10,... | collective-permute-start | bytes 294920 | tf_op jit(solution)/shard_map/ppermute | solution.py:178
  13.5 11.4 %collective-permute-start.3 = (bf16[4,6,16,128]{3,2,1,0:T(8,128)(2,1)}, bf16[4,6,16,128]{3,2,1,0:T(8,128)(2,1)S(1)}, u32[]{:S(2)}, u32[]{:S(2)}) collective-permute-start(bf16[4,6,16,128]{3,2,1,0:T(8,128)(2,1)} %get-tuple-element.34), channel_id=1, source_target_pairs={{0,7},{1,6},{2,5},{3,4},{4,3},{5,2},{6,1},{7,0},{8,15},{9,14},{10,... | collective-permute-start | bytes 294920 | tf_op jit(solution)/shard_map/ppermute | solution.py:178
  22.1 4.9 %collective-permute-start.4 = (bf16[4,6,16,128]{3,2,1,0:T(8,128)(2,1)}, bf16[4,6,16,128]{3,2,1,0:T(8,128)(2,1)S(1)}, u32[]{:S(2)}, u32[]{:S(2)}) collective-permute-start(bf16[4,6,16,128]{3,2,1,0:T(8,128)(2,1)} %get-tuple-element.35), channel_id=1, source_target_pairs={{0,2},{1,3},{2,0},{3,1},{4,6},{5,7},{6,4},{7,5},{8,10},{9,11},{10,... | collective-permute-start | bytes 294920 | tf_op jit(solution)/shard_map/ppermute | solution.py:178
  23.6 4.9 %collective-permute-start.5 = (bf16[4,6,16,128]{3,2,1,0:T(8,128)(2,1)}, bf16[4,6,16,128]{3,2,1,0:T(8,128)(2,1)S(1)}, u32[]{:S(2)}, u32[]{:S(2)}) collective-permute-start(bf16[4,6,16,128]{3,2,1,0:T(8,128)(2,1)} %get-tuple-element.36), channel_id=1, source_target_pairs={{0,3},{1,2},{2,1},{3,0},{4,7},{5,6},{6,5},{7,4},{8,11},{9,10},{10,... | collective-permute-start | bytes 294920 | tf_op jit(solution)/shard_map/ppermute | solution.py:178
  24.4 4.1 %collective-permute-start.6 = (bf16[4,6,16,128]{3,2,1,0:T(8,128)(2,1)}, bf16[4,6,16,128]{3,2,1,0:T(8,128)(2,1)S(1)}, u32[]{:S(2)}, u32[]{:S(2)}) collective-permute-start(bf16[4,6,16,128]{3,2,1,0:T(8,128)(2,1)} %get-tuple-element.37), channel_id=1, source_target_pairs={{0,1},{1,0},{2,3},{3,2},{4,5},{5,4},{6,7},{7,6},{8,9},{9,8},{10,11... | collective-permute-start | bytes 294920 | tf_op jit(solution)/shard_map/ppermute | solution.py:176
  37.9 39.1 %collective-permute-start.15 = (bf16[4,6,80,128]{3,2,1,0:T(8,128)(2,1)}, bf16[4,6,80,128]{3,2,1,0:T(8,128)(2,1)S(1)}, u32[]{:S(2)}, u32[]{:S(2)}) collective-permute-start(bf16[4,6,80,128]{3,2,1,0:T(8,128)(2,1)} %get-tuple-element.49), channel_id=1, source_target_pairs={{0,1},{1,0},{2,3},{3,2},{4,5},{5,4},{6,7},{7,6},{8,9},{9,8},{10,11... | collective-permute-start | bytes 1474568 | tf_op jit(solution)/shard_map/ppermute | solution.py:176
  38.5 1.5 %collective-permute-start.16 = (f32[4,128]{1,0:T(4,128)S(1)}, f32[4,128]{1,0:T(4,128)S(1)}, u32[]{:S(2)}, u32[]{:S(2)}) collective-permute-start(f32[4,128]{1,0:T(4,128)S(1)} %copy-done.16), channel_id=1, source_target_pairs={{0,1},{1,0},{2,3},{3,2},{4,5},{5,4},{6,7},{7,6},{8,9},{9,8},{10,11... | collective-permute-start | bytes 6152 | tf_op jit(solution)/shard_map/ppermute | solution.py:176
  40.0 5.9 %collective-permute-start.19 = (f32[4,128]{1,0:T(4,128)S(1)}, f32[4,128]{1,0:T(4,128)S(1)}, u32[]{:S(2)}, u32[]{:S(2)}) collective-permute-start(f32[4,128]{1,0:T(4,128)S(1)} %add.53), channel_id=1, source_target_pairs={{0,24},{8,16},{16,8},{24,0},{1,25},{9,17},{17,9},{25,1},{2,26},{10... | collective-permute-start | bytes 6152 | tf_op jit(solution)/shard_map/ppermute | solution.py:347
  42.7 3.6 %collective-permute-start.18 = (f32[4,128]{1,0:T(4,128)S(1)}, f32[4,128]{1,0:T(4,128)S(1)}, u32[]{:S(2)}, u32[]{:S(2)}) collective-permute-start(f32[4,128]{1,0:T(4,128)S(1)} %add.53), channel_id=1, source_target_pairs={{0,16},{8,24},{16,0},{24,8},{1,17},{9,25},{17,1},{25,9},{2,18},{10... | collective-permute-start | bytes 6152 | tf_op jit(solution)/shard_map/ppermute | solution.py:347
  43.2 6.7 %collective-permute-start.17 = (f32[4,128]{1,0:T(4,128)S(1)}, f32[4,128]{1,0:T(4,128)S(1)}, u32[]{:S(2)}, u32[]{:S(2)}) collective-permute-start(f32[4,128]{1,0:T(4,128)S(1)} %add.53), channel_id=1, source_target_pairs={{0,8},{8,0},{16,24},{24,16},{1,9},{9,1},{17,25},{25,17},{2,10},{10... | collective-permute-start | bytes 6152 | tf_op jit(solution)/shard_map/ppermute | solution.py:347
  43.5 23.3 %collective-permute-start.8 = (bf16[4,6,16,128]{3,2,1,0:T(8,128)(2,1)}, bf16[4,6,16,128]{3,2,1,0:T(8,128)(2,1)S(1)}, u32[]{:S(2)}, u32[]{:S(2)}) collective-permute-start(bf16[4,6,16,128]{3,2,1,0:T(8,128)(2,1)} %get-tuple-element.41), channel_id=1, source_target_pairs={{0,4},{1,5},{2,6},{3,7},{4,0},{5,1},{6,2},{7,3},{8,12},{9,13},{10,... | collective-permute-start | bytes 294920 | tf_op jit(solution)/shard_map/ppermute | solution.py:178
  45.9 22.4 %collective-permute-start.9 = (bf16[4,6,16,128]{3,2,1,0:T(8,128)(2,1)}, bf16[4,6,16,128]{3,2,1,0:T(8,128)(2,1)S(1)}, u32[]{:S(2)}, u32[]{:S(2)}) collective-permute-start(bf16[4,6,16,128]{3,2,1,0:T(8,128)(2,1)} %get-tuple-element.42), channel_id=1, source_target_pairs={{0,5},{1,4},{2,7},{3,6},{4,1},{5,0},{6,3},{7,2},{8,13},{9,12},{10,... | collective-permute-start | bytes 294920 | tf_op jit(solution)/shard_map/ppermute | solution.py:178
  46.3 24.3 %collective-permute-start.10 = (bf16[4,6,16,128]{3,2,1,0:T(8,128)(2,1)}, bf16[4,6,16,128]{3,2,1,0:T(8,128)(2,1)S(1)}, u32[]{:S(2)}, u32[]{:S(2)}) collective-permute-start(bf16[4,6,16,128]{3,2,1,0:T(8,128)(2,1)} %get-tuple-element.43), channel_id=1, source_target_pairs={{0,6},{1,7},{2,4},{3,5},{4,2},{5,3},{6,0},{7,1},{8,14},{9,15},{10,... | collective-permute-start | bytes 294920 | tf_op jit(solution)/shard_map/ppermute | solution.py:178
  49.9 5.4 %collective-permute-start.22 = (f32[4,128]{1,0:T(4,128)S(1)}, f32[4,128]{1,0:T(4,128)S(1)}, u32[]{:S(2)}, u32[]{:S(2)}) collective-permute-start(f32[4,128]{1,0:T(4,128)S(1)} %add_add_fusion), channel_id=1, source_target_pairs={{0,6},{2,4},{4,2},{6,0},{1,7},{3,5},{5,3},{7,1},{8,14},{10,12},{12... | collective-permute-start | bytes 6152 | tf_op jit(solution)/shard_map/ppermute | solution.py:347
  55.4 7.8 %collective-permute-start.21 = (f32[4,128]{1,0:T(4,128)S(1)}, f32[4,128]{1,0:T(4,128)S(1)}, u32[]{:S(2)}, u32[]{:S(2)}) collective-permute-start(f32[4,128]{1,0:T(4,128)S(1)} %add_add_fusion), channel_id=1, source_target_pairs={{0,4},{2,6},{4,0},{6,2},{1,5},{3,7},{5,1},{7,3},{8,12},{10,14},{12... | collective-permute-start | bytes 6152 | tf_op jit(solution)/shard_map/ppermute | solution.py:347
  63.2 3.6 %collective-permute-start.20 = (f32[4,128]{1,0:T(4,128)S(1)}, f32[4,128]{1,0:T(4,128)S(1)}, u32[]{:S(2)}, u32[]{:S(2)}) collective-permute-start(f32[4,128]{1,0:T(4,128)S(1)} %add_add_fusion), channel_id=1, source_target_pairs={{0,2},{2,0},{4,6},{6,4},{1,3},{3,1},{5,7},{7,5},{8,10},{10,8},{12,... | collective-permute-start | bytes 6152 | tf_op jit(solution)/shard_map/ppermute | solution.py:347
  66.8 6.3 %collective-permute-start.11 = (bf16[4,6,16,128]{3,2,1,0:T(8,128)(2,1)}, bf16[4,6,16,128]{3,2,1,0:T(8,128)(2,1)S(1)}, u32[]{:S(2)}, u32[]{:S(2)}) collective-permute-start(bf16[4,6,16,128]{3,2,1,0:T(8,128)(2,1)} %get-tuple-element.44), channel_id=1, source_target_pairs={{0,7},{1,6},{2,5},{3,4},{4,3},{5,2},{6,1},{7,0},{8,15},{9,14},{10,... | collective-permute-start | bytes 294920 | tf_op jit(solution)/shard_map/ppermute | solution.py:178
  66.8 10.2 %copy-start.9 = (bf16[4,6,16,128]{3,2,1,0:T(8,128)(2,1)}, bf16[4,6,16,128]{3,2,1,0:T(8,128)(2,1)S(1)}, u32[]{:S(2)}) copy-start(bf16[4,6,16,128]{3,2,1,0:T(8,128)(2,1)S(1)} %collective-permute-done.8.refs_1_) | copy-start | bytes 294916
  66.8 7.7 %collective-permute-start.12 = (bf16[4,6,16,128]{3,2,1,0:T(8,128)(2,1)}, bf16[4,6,16,128]{3,2,1,0:T(8,128)(2,1)S(1)}, u32[]{:S(2)}, u32[]{:S(2)}) collective-permute-start(bf16[4,6,16,128]{3,2,1,0:T(8,128)(2,1)} %get-tuple-element.45), channel_id=1, source_target_pairs={{0,2},{1,3},{2,0},{3,1},{4,6},{5,7},{6,4},{7,5},{8,10},{9,11},{10,... | collective-permute-start | bytes 294920 | tf_op jit(solution)/shard_map/ppermute | solution.py:178
  68.2 8.7 %collective-permute-start.13 = (bf16[4,6,16,128]{3,2,1,0:T(8,128)(2,1)}, bf16[4,6,16,128]{3,2,1,0:T(8,128)(2,1)S(1)}, u32[]{:S(2)}, u32[]{:S(2)}) collective-permute-start(bf16[4,6,16,128]{3,2,1,0:T(8,128)(2,1)} %get-tuple-element.46), channel_id=1, source_target_pairs={{0,3},{1,2},{2,1},{3,0},{4,7},{5,6},{6,5},{7,4},{8,11},{9,10},{10,... | collective-permute-start | bytes 294920 | tf_op jit(solution)/shard_map/ppermute | solution.py:178
  70.7 6.3 %collective-permute-start.14 = (bf16[4,6,16,128]{3,2,1,0:T(8,128)(2,1)}, bf16[4,6,16,128]{3,2,1,0:T(8,128)(2,1)S(1)}, u32[]{:S(2)}, u32[]{:S(2)}) collective-permute-start(bf16[4,6,16,128]{3,2,1,0:T(8,128)(2,1)} %get-tuple-element.47), channel_id=1, source_target_pairs={{0,1},{1,0},{2,3},{3,2},{4,5},{5,4},{6,7},{7,6},{8,9},{9,8},{10,11... | collective-permute-start | bytes 294920 | tf_op jit(solution)/shard_map/ppermute | solution.py:176
  (16 other events, 47.5 us)
